TPU v7x, 128 devices: a whole 4x4x4 slice. The times are simulated.
128 devices in a mesh: dom: 128 (over z, y, x, core).
Axes of the slice: x: 4, y: 4, z: 4, core: 2. Of those that a mesh axis runs over, the one named last changes fastest.
Arguments:
- features: bfloat16 [131072, 256], P('dom'), may hold values from -6 to 6
- edge_source: int32 [128, 128, 128], P('dom'), may hold values from 0 to 5119, as said below
- edge_relation: int32 [128, 128, 128], P('dom'), may hold values from 0 to 7
- edge_target: int32 [128, 128, 128], P('dom'), may hold values from 0 to 1023, as said below
- block_count: int32 [128], P('dom'), may hold values from 1 to 128, as said below
- send_list: int32 [128, 128, 32], P('dom'), may hold values from 0 to 1023
- bases_first: bfloat16 [30, 256, 256], P(None, 'dom'), may hold values from -0.375 to 0.375
- self_first: bfloat16 [256, 256], P('dom'), may hold values from -0.375 to 0.375
- coef_first: float32 [8, 30], replicated, may hold values from -1 to 1
- bias_first: float32 [256], replicated, may hold values from -3 to 3
- bases_second: bfloat16 [30, 256, 256], P(None, 'dom'), may hold values from -0.375 to 0.375
- self_second: bfloat16 [256, 256], P('dom'), may hold values from -0.375 to 0.375
- coef_second: float32 [8, 30], replicated, may hold values from -1 to 1
- bias_second: float32 [256], replicated, may hold values from -3 to 3
Outputs:
- embedded: bfloat16 [131072, 256], P('dom')
Inputs may be any that keep to these rules, and one draw needn't show every extreme that they name: `edge_source`: an entry below 1024 names a row of the edge's own partition; an entry 1024 + p * 32 + s names the row that partition p sends to the edge's partition in slot s, and p is never the edge's own partition. `edge_target`: non-decreasing within each block; all targets of one block lie in one aligned window of 16 rows, from 16 * k to 16 * k + 15 for some k. `block_count`: blocks at and beyond it are ignored; some partition uses all 128.
All inputs are finite; a program needn't handle non-finite values.
Results may differ from a plain program's by a relative error of at most 0.0064.
Values may be sent and summed in bfloat16 or wider, within the bound.
A program may use at most 128 MiB of HBM per device.

v0:
```python
import functools

import jax
import jax.numpy as jnp
from jax import lax
from jax.experimental import pallas as pl
from jax.experimental.pallas import tpu as pltpu
from jax.sharding import PartitionSpec as P

WIN = 16
LANES = 128
VMEM = pl.BlockSpec(memory_space=pltpu.VMEM)
SMEM = pl.BlockSpec(memory_space=pltpu.SMEM)
LIMIT = 60 * 1024 * 1024


def compose_weights(coef, bases):
    mixed = jnp.einsum(
        "rb,bij->rij", coef, bases.astype(jnp.float32), precision=lax.Precision.HIGHEST
    )
    return mixed.astype(jnp.bfloat16)


def layer_weights(bases, self_weight, coef):
    stacked = jnp.concatenate([compose_weights(coef, bases), self_weight[None]], axis=0)
    return lax.all_gather(stacked, "dom", axis=1, tiled=True)


def pick_rows(send_ref, rows_ref, out_ref):
    peers, slots = send_ref.shape
    nodes, width = rows_ref.shape
    group = 8

    def step(g, carry):
        ids = send_ref[pl.ds(pl.multiple_of(g * group, group), group), :]
        hot = (
            ids[:, :, None]
            == lax.broadcasted_iota(jnp.int32, (group, slots, nodes), 2)
        ).astype(jnp.float32).astype(jnp.bfloat16).reshape(group * slots, nodes)
        got = jnp.dot(hot, rows_ref[...], preferred_element_type=jnp.float32)
        out_ref[pl.ds(g * group, group)] = got.astype(jnp.bfloat16).reshape(group, slots, width)
        return carry

    lax.fori_loop(0, peers // group, step, 0)


def outgoing_rows(send_rows, rows):
    peers, slots = send_rows.shape
    return pl.pallas_call(
        pick_rows,
        out_shape=jax.ShapeDtypeStruct((peers, slots, rows.shape[1]), jnp.bfloat16),
        in_specs=[VMEM, VMEM],
        out_specs=VMEM,
        compiler_params=pltpu.CompilerParams(vmem_limit_bytes=LIMIT),
        name="outgoing_rows",
    )(send_rows, rows)


def layer_body(
    relu,
    count_ref,
    window_ref,
    source_ref,
    slot_ref,
    own_ref,
    recv_ref,
    weight_ref,
    bias_ref,
    out_ref,
    table,
    pooled,
    counts,
    stage_a,
    stage_b,
):
    nodes, width = own_ref.shape
    relations = weight_ref.shape[0] - 1
    block_width = slot_ref.shape[1]
    slots = WIN * relations
    chunk = 256

    def fill(src_ref, base):
        def step(i, carry):
            rows = src_ref[pl.ds(pl.multiple_of(i * chunk, chunk), chunk), :].astype(jnp.float32)
            at = pl.multiple_of(base + i * 2 * chunk, 2 * chunk)
            table[pl.ds(at, chunk, stride=2), :] = rows[:, :LANES]
            table[pl.ds(at + 1, chunk, stride=2), :] = rows[:, LANES:]
            return carry

        lax.fori_loop(0, src_ref.shape[0] // chunk, step, 0)

    fill(own_ref, 0)
    fill(recv_ref, 2 * nodes)

    def clear(i, carry):
        at = pl.multiple_of(i * slots, slots)
        pooled[pl.ds(at, slots), :] = jnp.zeros((slots, width), jnp.float32)
        counts[pl.ds(at, slots), :] = jnp.zeros((slots, LANES), jnp.float32)
        return carry

    lax.fori_loop(0, nodes // WIN, clear, 0)

    def gather(block, stage):
        for e in range(block_width):
            at = pl.multiple_of(source_ref[block, e], 2)
            stage[pl.ds(2 * e, 2), :] = table[pl.ds(at, 2), :]

    def pool(block, stage):
        hot = (
            slot_ref[pl.ds(block, 1), :]
            == lax.broadcasted_iota(jnp.int32, (slots, block_width), 0)
        ).astype(jnp.float32).astype(jnp.bfloat16)
        left = stage[pl.ds(0, block_width, stride=2), :].astype(jnp.bfloat16)
        right = stage[pl.ds(1, block_width, stride=2), :].astype(jnp.bfloat16)
        ones = jnp.ones((block_width, LANES), jnp.bfloat16)
        at = pl.multiple_of(window_ref[block] * slots, slots)
        rows = pl.ds(at, slots)
        pooled[rows, :LANES] += jnp.dot(hot, left, preferred_element_type=jnp.float32)
        pooled[rows, LANES:] += jnp.dot(hot, right, preferred_element_type=jnp.float32)
        counts[rows, :] += jnp.dot(hot, ones, preferred_element_type=jnp.float32)

    used = count_ref[0]

    def pair(i, carry):
        gather(2 * i, stage_a)
        pool(2 * i, stage_a)
        gather(2 * i + 1, stage_b)
        pool(2 * i + 1, stage_b)
        return carry

    lax.fori_loop(0, (used + 1) // 2, pair, 0)

    part = 256
    windows = part // WIN

    def finish(i, carry):
        at = pl.multiple_of(i * part, part)
        total = jnp.dot(
            own_ref[pl.ds(at, part), :], weight_ref[relations], preferred_element_type=jnp.float32
        ) + bias_ref[...]
        base = pl.multiple_of(i * windows * slots, windows * slots)
        sums = pooled[pl.ds(base, windows * slots), :].reshape(windows, relations, WIN, width)
        tally = counts[pl.ds(base, windows * slots), :].reshape(windows, relations, WIN, LANES)
        for r in range(relations):
            inverse = 1.0 / jnp.maximum(tally[:, r].reshape(part, LANES), 1.0)
            sums_r = sums[:, r].reshape(part, width)
            mean = jnp.concatenate(
                [sums_r[:, :LANES] * inverse, sums_r[:, LANES:] * inverse], axis=1
            ).astype(jnp.bfloat16)
            total = total + jnp.dot(mean, weight_ref[r], preferred_element_type=jnp.float32)
        if relu:
            total = jnp.maximum(total, 0.0)
        out_ref[pl.ds(at, part), :] = total.astype(jnp.bfloat16)
        return carry

    lax.fori_loop(0, nodes // part, finish, 0)


def relational_layer(relu, rows, received, count, windows, sources, slot_ids, weights, bias):
    nodes, width = rows.shape
    relations = weights.shape[0] - 1
    table_rows = 2 * (nodes + received.shape[0])
    return pl.pallas_call(
        functools.partial(layer_body, relu),
        out_shape=jax.ShapeDtypeStruct((nodes, width), jnp.bfloat16),
        in_specs=[SMEM, SMEM, SMEM, VMEM, VMEM, VMEM, VMEM, VMEM],
        out_specs=VMEM,
        scratch_shapes=[
            pltpu.VMEM((table_rows, LANES), jnp.float32),
            pltpu.VMEM((nodes * relations, width), jnp.float32),
            pltpu.VMEM((nodes * relations, LANES), jnp.float32),
            pltpu.VMEM((2 * LANES, LANES), jnp.float32),
            pltpu.VMEM((2 * LANES, LANES), jnp.float32),
        ],
        compiler_params=pltpu.CompilerParams(vmem_limit_bytes=LIMIT),
        name="relational_layer",
    )(count, windows, sources, slot_ids, rows, received, weights, bias.reshape(1, width))


def shards(
    features,
    edge_source,
    edge_relation,
    edge_target,
    block_count,
    send_list,
    bases_first,
    self_first,
    coef_first,
    bias_first,
    bases_second,
    self_second,
    coef_second,
    bias_second,
):
    sources = edge_source[0] * 2
    targets = edge_target[0]
    windows = targets[:, 0] // WIN
    blocks = targets.shape[0]
    in_use = lax.broadcasted_iota(jnp.int32, targets.shape, 0) < block_count[0]
    slot_ids = jnp.where(in_use, edge_relation[0] * WIN + targets % WIN, -1)
    send_rows = send_list[0]
    width = features.shape[1]

    def exchange(rows):
        out = outgoing_rows(send_rows, rows)
        incoming = lax.all_to_all(out, "dom", split_axis=0, concat_axis=0, tiled=True)
        return incoming.reshape(-1, width)

    first_weights = layer_weights(bases_first, self_first, coef_first)
    second_weights = layer_weights(bases_second, self_second, coef_second)
    hidden = relational_layer(
        True, features, exchange(features), block_count, windows, sources, slot_ids,
        first_weights, bias_first,
    )
    return relational_layer(
        False, hidden, exchange(hidden), block_count, windows, sources, slot_ids,
        second_weights, bias_second,
    )


def solution(mesh):
    placed = (
        P("dom", None),
        P("dom", None, None),
        P("dom", None, None),
        P("dom", None, None),
        P("dom"),
        P("dom", None, None),
        P(None, "dom", None),
        P("dom", None),
        P(),
        P(),
        P(None, "dom", None),
        P("dom", None),
        P(),
        P(),
    )
    return jax.shard_map(
        shards, mesh=mesh, in_specs=placed, out_specs=P("dom", None), check_vma=False
    )
```

profile of v0, /device:TPU:86, one launch (start us, length us, event | category | flops | bytes accessed | tf_op | source)
XLA Modules:
  0.0 210.9 jit_solution(7713457609027302151)
XLA Ops:
  6.5 0.0 copy-start
  6.5 0.0 all-gather.3.cloned.1.call-start
  6.5 0.7 copy.32
  7.2 0.1 copy-done
  7.3 0.8 convolution_convert_fusion.1
  8.1 0.6 pad_maximum_fusion
  8.7 0.0 all-gather.3.cloned.1.call-update
  8.7 1.4 copy.30
  10.2 8.7 %outgoing_rows.2 = bf16[128,32,256]{2,1,0:T(8,128)(2,1)} custom-call(s32[128,32]{1,0:T(8,128)} %bitcast.23, bf16[1024,256]{1,0:T(8,128)(2,1)} %own_ref.1), custom_call_target="tpu_custom_call" | custom-call | tf_op jit(solution)/shard_map/outgoing_rows/pallas_call | solution.py:49
  18.9 0.0 copy-start.8
  18.9 0.0 copy-start.6
  18.9 0.0 copy-start.7
  18.9 0.0 copy-start.3
  18.9 0.0 copy-start.5
  18.9 0.0 copy-start.4
  18.9 9.9 %all-to-all-start = ((bf16[128,32,256]{2,1,0:T(8,128)(2,1)}), bf16[128,32,256]{2,1,0:T(8,128)(2,1)S(1)}, u32[]{:S(2)}, u32[]{:S(2)}) async-start(bf16[128,32,256]{2,1,0:T(8,128)(2,1)} %outgoing_rows.2), calls=%async_computation | async-start | bytes 4194304 | tf_op jit(solution)/shard_map/all_to_all | solution.py:207
  28.9 0.0 all-gather.5.cloned.1.call-start
  28.9 0.0 copy-done.8
  28.9 0.0 copy-done.6
  29.0 0.0 copy-done.7
  29.0 0.1 convolution_convert_fusion
  29.1 0.6 pad_maximum_fusion.1
  29.7 0.0 all-gather.5.cloned.1.call-update
  30.4 0.0 copy-done.3
  30.4 0.1 slice_reduce_fusion
  30.5 0.6 and_select_fusion.window_ref
  31.1 0.0 copy-done.5
  31.1 0.6 multiply_bitcast_fusion.source_ref
  31.7 0.0 copy-done.4
  31.7 0.7 fusion.2.slot_ref
  32.4 49.4 %all-gather.3.cloned.1.call-done = bf16[9,256,256]{2,0,1:T(8,128)(2,1)} async-done(((bf16[9,2,256]{2,0,1:T(8,128)(2,1)}), bf16[9,256,256]{2,0,1:T(8,128)(2,1)}) %all-gather.3.cloned.1.call-update) | async-done | bytes 1179664 | tf_op jit(solution)/shard_map/all_gather | solution.py:26
  81.9 3.0 %copy.33.weight_ref = bf16[9,256,256]{2,1,0:T(8,128)(2,1)} copy(bf16[9,256,256]{2,0,1:T(8,128)(2,1)} %all-gather.3.cloned.1.call-done) | data formatting | bytes 2359296 | tf_op jit(solution)/shard_map/all_gather | solution.py:26
  84.9 0.0 all-to-all-done
  84.9 0.0 copy-start.1
  84.9 1.3 copy-done.1
  86.2 33.7 %relational_layer.2.rows_ref.own_ref = bf16[1024,256]{1,0:T(8,128)(2,1)} custom-call(s32[1]{0:T(128)} %copy.41.count_ref, s32[128]{0:T(128)} %and_select_fusion.window_ref, s32[128,128]{1,0:T(8,128)} %multiply_bitcast_fusion.source_ref, s32[128,128]{1,0:T(8,128)} %fusion.2.slot_ref, bf16[1024,256]{1,0:T(8,128)(2,1)} %own_ref.1, bf16[4096,256]{1,0:T(8,128)(2,1)} %bitcast.21, ...), custom_call_target="tpu_custom_call" | custom-call | tf_op jit(solution)/shard_map/relational_layer/pallas_call | solution.py:163
  119.9 8.7 %outgoing_rows.3 = bf16[128,32,256]{2,1,0:T(8,128)(2,1)} custom-call(s32[128,32]{1,0:T(8,128)} %bitcast.24, bf16[1024,256]{1,0:T(8,128)(2,1)} %relational_layer.2.rows_ref.own_ref), custom_call_target="tpu_custom_call" | custom-call | tf_op jit(solution)/shard_map/outgoing_rows/pallas_call | solution.py:49
  128.6 9.5 %all-to-all-start.1 = ((bf16[128,32,256]{2,1,0:T(8,128)(2,1)}), bf16[128,32,256]{2,1,0:T(8,128)(2,1)S(1)}, u32[]{:S(2)}, u32[]{:S(2)}) async-start(bf16[128,32,256]{2,1,0:T(8,128)(2,1)} %outgoing_rows.3), calls=%async_computation.1 | async-start | bytes 4194304 | tf_op jit(solution)/shard_map/all_to_all | solution.py:207
  138.1 27.8 %all-gather.5.cloned.1.call-done = bf16[9,256,256]{2,0,1:T(8,128)(2,1)} async-done(((bf16[9,2,256]{2,0,1:T(8,128)(2,1)}), bf16[9,256,256]{2,0,1:T(8,128)(2,1)}) %all-gather.5.cloned.1.call-update) | async-done | bytes 1179664 | tf_op jit(solution)/shard_map/all_gather | solution.py:26
  166.0 3.1 %copy.36.weight_ref = bf16[9,256,256]{2,1,0:T(8,128)(2,1)} copy(bf16[9,256,256]{2,0,1:T(8,128)(2,1)} %all-gather.5.cloned.1.call-done) | data formatting | bytes 2359296 | tf_op jit(solution)/shard_map/all_gather | solution.py:26
  169.0 0.0 all-to-all-done.1
  169.0 0.0 copy-start.2
  169.0 1.3 copy-done.2
  170.4 33.7 %relational_layer.3 = bf16[1024,256]{1,0:T(8,128)(2,1)} custom-call(s32[1]{0:T(128)} %copy.41.count_ref, s32[128]{0:T(128)} %and_select_fusion.window_ref, s32[128,128]{1,0:T(8,128)} %multiply_bitcast_fusion.source_ref, s32[128,128]{1,0:T(8,128)} %fusion.2.slot_ref, bf16[1024,256]{1,0:T(8,128)(2,1)} %relational_layer.2.rows_ref.own_ref, ...), custom_call_target="tpu_custom_call" | custom-call | tf_op jit(solution)/shard_map/relational_layer/pallas_call | solution.py:163
  (2 shorter events, 0.0 us)
Async XLA Ops:
  6.5 0.8 copy-start
  6.5 75.3 %all-gather.3.cloned.1.call-start = ((), (), s32[]{:S(2)}) async-start(), calls=%async_computation.2 | async-start | bytes 2113536 | tf_op jit(solution)/shard_map/all_gather | solution.py:26
  18.9 10.0 %copy-start.8 = (bf16[2,256]{1,0:T(2,128)(2,1)S(1)}, bf16[2,256]{1,0:T(2,128)(2,1)}, u32[]{:S(2)}) copy-start(bf16[2,256]{1,0:T(2,128)(2,1)} %param.25) | copy-start | bytes 3076
  18.9 10.0 %copy-start.6 = (bf16[30,2,256]{2,1,0:T(2,128)(2,1)S(1)}, bf16[30,2,256]{2,1,0:T(2,128)(2,1)}, u32[]{:S(2)}) copy-start(bf16[30,2,256]{2,1,0:T(2,128)(2,1)} %param.24) | copy-start | bytes 92164
  18.9 10.0 %copy-start.7 = (f32[8,30]{1,0:T(8,128)S(1)}, f32[8,30]{1,0:T(8,128)}, u32[]{:S(2)}) copy-start(f32[8,30]{1,0:T(8,128)} %param.26) | copy-start | bytes 2884
  18.9 11.5 %copy-start.3 = (s32[1,128,128]{2,1,0:T(8,128)S(1)}, s32[1,128,128]{2,1,0:T(8,128)}, u32[]{:S(2)}) copy-start(s32[1,128,128]{2,1,0:T(8,128)} %param.17) | copy-start | bytes 196612
  18.9 12.2 %copy-start.5 = (s32[1,128,128]{2,1,0:T(8,128)S(1)}, s32[1,128,128]{2,1,0:T(8,128)}, u32[]{:S(2)}) copy-start(s32[1,128,128]{2,1,0:T(8,128)} %param.15) | copy-start | bytes 196612
  18.9 12.8 %copy-start.4 = (s32[1,128,128]{2,1,0:T(8,128)S(1)}, s32[1,128,128]{2,1,0:T(8,128)}, u32[]{:S(2)}) copy-start(s32[1,128,128]{2,1,0:T(8,128)} %param.16) | copy-start | bytes 196612
  18.9 66.0 %all-to-all-start = ((bf16[128,32,256]{2,1,0:T(8,128)(2,1)}), bf16[128,32,256]{2,1,0:T(8,128)(2,1)S(1)}, u32[]{:S(2)}, u32[]{:S(2)}) async-start(bf16[128,32,256]{2,1,0:T(8,128)(2,1)} %outgoing_rows.2), calls=%async_computation | async-start | bytes 4194304 | tf_op jit(solution)/shard_map/all_to_all | solution.py:207
  28.9 137.1 %all-gather.5.cloned.1.call-start = ((), (), s32[]{:S(2)}) async-start(), calls=%async_computation.3 | async-start | bytes 2113536 | tf_op jit(solution)/shard_map/all_gather | solution.py:26
  84.9 1.3 copy-start.1
  128.6 40.4 %all-to-all-start.1 = ((bf16[128,32,256]{2,1,0:T(8,128)(2,1)}), bf16[128,32,256]{2,1,0:T(8,128)(2,1)S(1)}, u32[]{:S(2)}, u32[]{:S(2)}) async-start(bf16[128,32,256]{2,1,0:T(8,128)(2,1)} %outgoing_rows.3), calls=%async_computation.1 | async-start | bytes 4194304 | tf_op jit(solution)/shard_map/all_to_all | solution.py:207
  169.0 1.3 copy-start.2
Sparse Core Ops, SparseCore 0:
  10.5 71.3 all-gather.2
  85.0 80.9 all-gather.4
where the time goes:
time: 211 us
  Pallas kernels  84.8 us (40%)
  waiting for transfers between devices  77.3 us (37%)
  starting transfers between devices  19.4 us (9%)
  between operations  14.1 us (7%)
  local copies, waits for them, and re-layouts  11.1 us (5%)
  other arithmetic  3.16 us (1%)
    all_gather x2, waiting for transfers between devices, layer_weights(): return lax.all_gather(stacked, 'dom', axis=1, tiled=True)  77.3 us
    pallas_call x2, Pallas kernels, relational_layer(): pl.pallas_call(functools.partial(layer_body, relu), out_shape=jax.ShapeDt...  67.4 us
    all_to_all x2, starting transfers between devices, exchange(): lax.all_to_all(out, 'dom', split_axis=0, concat_axis=0, tiled=True)  19.4 us
    pallas_call x2, Pallas kernels, outgoing_rows(): pl.pallas_call(pick_rows, out_shape=jax.ShapeDtypeStruct((peers, slots, r...  17.4 us
    all_gather x2, local copies, waits for them, and re-layouts, layer_weights(): return lax.all_gather(stacked, 'dom', axis=1, tiled=True)  6.09 us
  transfers between devices with their start and end apart: 4, of which 2 were waited for; matrix products, arithmetic and copies ran while one was open for 5% of the time, Pallas kernels for 24%

commit v1 on v0

--- a/solution.py
+++ b/solution.py
@@ -21,9 +21,11 @@
     return mixed.astype(jnp.bfloat16)
 
 
-def layer_weights(bases, self_weight, coef):
+def weight_part(bases, self_weight, coef):
     stacked = jnp.concatenate([compose_weights(coef, bases), self_weight[None]], axis=0)
-    return lax.all_gather(stacked, "dom", axis=1, tiled=True)
+    matrices, pair, width = stacked.shape
+    split = stacked.reshape(matrices, pair, width // LANES, LANES).transpose(0, 2, 1, 3)
+    return split[:, :, None]
 
 
 def pick_rows(send_ref, rows_ref, out_ref):
@@ -54,6 +56,178 @@
         compiler_params=pltpu.CompilerParams(vmem_limit_bytes=LIMIT),
         name="outgoing_rows",
     )(send_rows, rows)
+
+
+MESH = pl.DeviceIdType.MESH
+ANY = pl.BlockSpec(memory_space=pl.ANY)
+BATCHES = (6, 6, 14, 14, 28, 28, 31)
+
+
+def greet(me, count):
+    barrier = pltpu.get_barrier_semaphore()
+
+    def signal(k, carry):
+        pl.semaphore_signal(
+            barrier, inc=1, device_id=(lax.rem(me + k, count),), device_id_type=MESH
+        )
+        return carry
+
+    lax.fori_loop(1, count, signal, 0)
+    pl.semaphore_wait(barrier, count - 1)
+
+
+def send_blocks(me, count, first, last, out_ref, in_ref, send_sem, recv_sem):
+    def send(k, carry):
+        to = lax.rem(me + lax.rem(k * 37, count), count)
+        pltpu.make_async_remote_copy(
+            src_ref=out_ref.at[to],
+            dst_ref=in_ref.at[me],
+            send_sem=send_sem,
+            recv_sem=recv_sem,
+            device_id=(to,),
+            device_id_type=MESH,
+        ).start()
+        return carry
+
+    lax.fori_loop(first, last, send, 0)
+
+
+def drain_blocks(count, out_ref, in_ref, send_sem, recv_sem):
+    some = pl.ds(0, count - 1)
+    pltpu.make_async_copy(in_ref.at[some], in_ref.at[some], recv_sem).wait()
+    pltpu.make_async_copy(out_ref.at[some], out_ref.at[some], send_sem).wait()
+
+
+def exchange_body(count, out_ref, in_ref, send_sem, recv_sem, own_sem):
+    me = lax.axis_index("dom")
+    own = pltpu.make_async_copy(out_ref.at[me], in_ref.at[me], own_sem)
+    own.start()
+    greet(me, count)
+    send_blocks(me, count, 1, count, out_ref, in_ref, send_sem, recv_sem)
+    own.wait()
+    drain_blocks(count, out_ref, in_ref, send_sem, recv_sem)
+
+
+def exchange_gather_body(
+    count,
+    out_ref,
+    part_ref,
+    in_ref,
+    full_ref,
+    send_sem,
+    recv_sem,
+    own_sem,
+    part_sem,
+    hop_send,
+    hop_recv,
+):
+    me = lax.axis_index("dom")
+    core = lax.rem(me, 2)
+    other = me + 1 - 2 * core
+    own = pltpu.make_async_copy(out_ref.at[me], in_ref.at[me], own_sem)
+    own.start()
+    mine = pltpu.make_async_copy(
+        part_ref.at[core], full_ref.at[core, :, :, pl.ds(me, 1)], part_sem
+    )
+    mine.start()
+    greet(me, count)
+
+    started = []
+
+    def hop(index, src, dst, to):
+        copy = pltpu.make_async_remote_copy(
+            src_ref=src,
+            dst_ref=dst,
+            send_sem=hop_send.at[index],
+            recv_sem=hop_recv.at[index],
+            device_id=(to,),
+            device_id_type=MESH,
+        )
+        copy.start()
+        started.append(copy)
+        return copy
+
+    sent = 1
+
+    def batch(stage):
+        nonlocal sent
+        last = sent + BATCHES[stage]
+        send_blocks(me, count, sent, last, out_ref, in_ref, send_sem, recv_sem)
+        sent = last
+
+    pair = hop(
+        0, part_ref.at[1 - core], full_ref.at[1 - core, :, :, pl.ds(me, 1)], other
+    )
+    batch(0)
+    mine.wait()
+    pair.wait_recv()
+    stage = 1
+    index = 1
+    for step in (2, 8, 32):
+        place = lax.rem(me // step, 4)
+        base = (me // (4 * step)) * (4 * step)
+        inner = lax.rem(me, step)
+
+        def at(p, half=None):
+            p = lax.rem(p + 8, 4)
+            size = step if half is None else step // 2
+            start = base + p * step + (0 if half is None else half * size)
+            return full_ref.at[core, :, :, pl.ds(start, size)]
+
+        def device(p):
+            return base + lax.rem(p + 8, 4) * step + inner
+
+        up = hop(index, at(place), at(place), device(place + 1))
+        down = hop(index + 1, at(place), at(place), device(place - 1))
+        batch(stage)
+        up.wait_recv()
+        down.wait_recv()
+        far_up = hop(index + 2, at(place - 1, 0), at(place - 1, 0), device(place + 1))
+        far_down = hop(index + 3, at(place + 1, 1), at(place + 1, 1), device(place - 1))
+        batch(stage + 1)
+        far_up.wait_recv()
+        far_down.wait_recv()
+        stage += 2
+        index += 4
+    last = hop(index, full_ref.at[core], full_ref.at[core], other)
+    last.wait_recv()
+    for copy in started:
+        copy.wait_send()
+    own.wait()
+    drain_blocks(count, out_ref, in_ref, send_sem, recv_sem)
+
+
+def exchange(out, count):
+    return pl.pallas_call(
+        functools.partial(exchange_body, count),
+        out_shape=jax.ShapeDtypeStruct(out.shape, out.dtype),
+        in_specs=[VMEM],
+        out_specs=VMEM,
+        scratch_shapes=[pltpu.SemaphoreType.DMA] * 3,
+        compiler_params=pltpu.CompilerParams(
+            collective_id=1, has_side_effects=True, vmem_limit_bytes=LIMIT
+        ),
+        name="exchange",
+    )(out)
+
+
+def exchange_gather(out, part, count):
+    layers, matrices, halves, _, pair, lanes = part.shape
+    return pl.pallas_call(
+        functools.partial(exchange_gather_body, count),
+        out_shape=(
+            jax.ShapeDtypeStruct(out.shape, out.dtype),
+            jax.ShapeDtypeStruct((layers, matrices, halves, count, pair, lanes), part.dtype),
+        ),
+        in_specs=[VMEM, VMEM],
+        out_specs=(VMEM, VMEM),
+        scratch_shapes=[pltpu.SemaphoreType.DMA] * 4
+        + [pltpu.SemaphoreType.DMA((14,)), pltpu.SemaphoreType.DMA((14,))],
+        compiler_params=pltpu.CompilerParams(
+            collective_id=0, has_side_effects=True, vmem_limit_bytes=LIMIT
+        ),
+        name="exchange_gather",
+    )(out, part)
 
 
 def layer_body(
@@ -135,9 +309,12 @@
 
     def finish(i, carry):
         at = pl.multiple_of(i * part, part)
-        total = jnp.dot(
-            own_ref[pl.ds(at, part), :], weight_ref[relations], preferred_element_type=jnp.float32
-        ) + bias_ref[...]
+        own = own_ref[pl.ds(at, part), :]
+        totals = [
+            jnp.dot(own, weight_ref[relations, h], preferred_element_type=jnp.float32)
+            + bias_ref[:, h * LANES : (h + 1) * LANES]
+            for h in range(2)
+        ]
         base = pl.multiple_of(i * windows * slots, windows * slots)
         sums = pooled[pl.ds(base, windows * slots), :].reshape(windows, relations, WIN, width)
         tally = counts[pl.ds(base, windows * slots), :].reshape(windows, relations, WIN, LANES)
@@ -147,7 +324,11 @@
             mean = jnp.concatenate(
                 [sums_r[:, :LANES] * inverse, sums_r[:, LANES:] * inverse], axis=1
             ).astype(jnp.bfloat16)
-            total = total + jnp.dot(mean, weight_ref[r], preferred_element_type=jnp.float32)
+            totals = [
+                totals[h] + jnp.dot(mean, weight_ref[r, h], preferred_element_type=jnp.float32)
+                for h in range(2)
+            ]
+        total = jnp.concatenate(totals, axis=1)
         if relu:
             total = jnp.maximum(total, 0.0)
         out_ref[pl.ds(at, part), :] = total.astype(jnp.bfloat16)
@@ -202,20 +383,23 @@
     send_rows = send_list[0]
     width = features.shape[1]
 
-    def exchange(rows):
-        out = outgoing_rows(send_rows, rows)
-        incoming = lax.all_to_all(out, "dom", split_axis=0, concat_axis=0, tiled=True)
-        return incoming.reshape(-1, width)
-
-    first_weights = layer_weights(bases_first, self_first, coef_first)
-    second_weights = layer_weights(bases_second, self_second, coef_second)
+    part = jnp.stack(
+        [
+            weight_part(bases_first, self_first, coef_first),
+            weight_part(bases_second, self_second, coef_second),
+        ]
+    )
+    count = send_rows.shape[0]
+    received, full = exchange_gather(outgoing_rows(send_rows, features), part, count)
+    full = full.reshape(full.shape[:3] + (width, LANES))
     hidden = relational_layer(
-        True, features, exchange(features), block_count, windows, sources, slot_ids,
-        first_weights, bias_first,
-    )
+        True, features, received.reshape(-1, width), block_count, windows, sources, slot_ids,
+        full[0], bias_first,
+    )
+    received = exchange(outgoing_rows(send_rows, hidden), count)
     return relational_layer(
-        False, hidden, exchange(hidden), block_count, windows, sources, slot_ids,
-        second_weights, bias_second,
+        False, hidden, received.reshape(-1, width), block_count, windows, sources, slot_ids,
+        full[1], bias_second,
     )
 
 

time: 211 us -> 193 us (0.915)
  the two profiles are of different devices: /device:TPU:86 before, /device:TPU:3 now
where the time goes in v1:
time: 193 us; the launch traced here: 192 us
  Pallas kernels  178 us (92%)
  local copies, waits for them, and re-layouts  8.48 us (4%)
  other arithmetic  3.32 us (2%)
    pallas_call x2, Pallas kernels, relational_layer(): pl.pallas_call(functools.partial(layer_body, relu), out_shape=jax.ShapeDt...  69.7 us
    pallas_call x1, Pallas kernels, exchange_gather(): pl.pallas_call(functools.partial(exchange_gather_body, count), out_shape=...  57.1 us
    pallas_call x1, Pallas kernels, exchange(): pl.pallas_call(functools.partial(exchange_body, count), out_shape=jax.Sha...  33.9 us
    pallas_call x2, Pallas kernels, outgoing_rows(): pl.pallas_call(pick_rows, out_shape=jax.ShapeDtypeStruct((peers, slots, r...  17.4 us
    slice x1, local copies, waits for them, and re-layouts, shards(): full[1]  6.11 us

profile of v1, /device:TPU:3, one launch (start us, length us, event | category | flops | bytes accessed | tf_op | source)
XLA Modules:
  0.0 192.3 jit_solution(11789410896651442039)
XLA Ops:
  0.0 0.0 copy-start
  0.0 0.8 copy-done
  0.8 0.8 convolution_convert_fusion.1
  1.6 0.9 convolution_convert_fusion
  2.5 0.7 maximum_bitcast_fusion
  3.3 0.6 pad_maximum_fusion.part_ref
  3.9 1.4 copy.18
  5.3 8.7 %outgoing_rows.2.out_ref = bf16[128,32,256]{2,1,0:T(8,128)(2,1)} custom-call(s32[128,32]{1,0:T(8,128)} %bitcast.39, bf16[1024,256]{1,0:T(8,128)(2,1)} %own_ref.1), custom_call_target="tpu_custom_call" | custom-call | tf_op jit(solution)/shard_map/outgoing_rows/pallas_call | solution.py:51
  14.1 57.1 %exchange_gather.1 = (bf16[128,32,256]{2,1,0:T(8,128)(2,1)}, bf16[2,9,2,128,2,128]{5,4,3,2,1,0:T(2,128)(2,1)}) custom-call(bf16[128,32,256]{2,1,0:T(8,128)(2,1)} %outgoing_rows.2.out_ref, bf16[2,9,2,1,2,128]{5,4,3,2,1,0:T(2,128)(2,1)} %pad_maximum_fusion.part_ref), custom_call_target="tpu_custom_call" | custom-call | tf_op jit(solution)/shard_map/exchange_gather/pallas_call | solution.py:216
  71.2 0.0 copy-start.1
  71.2 0.0 copy-start.2
  71.2 0.0 copy-start.3
  71.2 6.1 %fusion.7 = (bf16[1,9,2,128,2,128]{5,4,3,2,1,0:T(2,128)(2,1)}, bf16[1,9,2,128,2,128]{5,4,3,2,1,0:T(2,128)(2,1)}) fusion(bf16[2,9,2,128,2,128]{5,4,3,2,1,0:T(2,128)(2,1)} %get-tuple-element.8), kind=kLoop, calls=%fused_computation.22 | loop fusion | bytes 4718592 | tf_op jit(solution)/shard_map/slice | solution.py:402
  78.0 0.0 copy-done.1
  78.0 0.0 copy-done.2
  78.0 0.7 fusion.2.slot_ref
  78.7 0.0 copy-done.3
  78.7 0.6 multiply_bitcast_fusion.source_ref
  79.4 0.1 slice_reduce_fusion
  79.5 0.6 and_select_fusion.window_ref
  80.1 34.8 %relational_layer.2.rows_ref.own_ref = bf16[1024,256]{1,0:T(8,128)(2,1)} custom-call(s32[1]{0:T(128)} %copy.27.count_ref, s32[128]{0:T(128)} %and_select_fusion.window_ref, s32[128,128]{1,0:T(8,128)} %multiply_bitcast_fusion.source_ref, s32[128,128]{1,0:T(8,128)} %fusion.2.slot_ref, bf16[1024,256]{1,0:T(8,128)(2,1)} %own_ref.1, bf16[4096,256]{1,0:T(8,128)(2,1)} %bitcast.38, ...), custom_call_target="tpu_custom_call" | custom-call | tf_op jit(solution)/shard_map/relational_layer/pallas_call | solution.py:344
  114.9 8.7 %outgoing_rows.3.out_ref = bf16[128,32,256]{2,1,0:T(8,128)(2,1)} custom-call(s32[128,32]{1,0:T(8,128)} %bitcast.40, bf16[1024,256]{1,0:T(8,128)(2,1)} %relational_layer.2.rows_ref.own_ref), custom_call_target="tpu_custom_call" | custom-call | tf_op jit(solution)/shard_map/outgoing_rows/pallas_call | solution.py:51
  123.6 33.9 %exchange.1 = bf16[128,32,256]{2,1,0:T(8,128)(2,1)} custom-call(bf16[128,32,256]{2,1,0:T(8,128)(2,1)} %outgoing_rows.3.out_ref), custom_call_target="tpu_custom_call" | custom-call | tf_op jit(solution)/shard_map/exchange/pallas_call | solution.py:201
  157.5 34.8 %relational_layer.3 = bf16[1024,256]{1,0:T(8,128)(2,1)} custom-call(s32[1]{0:T(128)} %copy.27.count_ref, s32[128]{0:T(128)} %and_select_fusion.window_ref, s32[128,128]{1,0:T(8,128)} %multiply_bitcast_fusion.source_ref, s32[128,128]{1,0:T(8,128)} %fusion.2.slot_ref, bf16[1024,256]{1,0:T(8,128)(2,1)} %relational_layer.2.rows_ref.own_ref, ...), custom_call_target="tpu_custom_call" | custom-call | tf_op jit(solution)/shard_map/relational_layer/pallas_call | solution.py:344
  (5 shorter events, 0.1 us)
Async XLA Ops:
  0.0 0.8 copy-start
  71.2 6.8 %copy-start.1 = (s32[1,128,128]{2,1,0:T(8,128)S(1)}, s32[1,128,128]{2,1,0:T(8,128)}, u32[]{:S(2)}) copy-start(s32[1,128,128]{2,1,0:T(8,128)} %param.17) | copy-start | bytes 196612
  71.2 6.8 %copy-start.2 = (s32[1,128,128]{2,1,0:T(8,128)S(1)}, s32[1,128,128]{2,1,0:T(8,128)}, u32[]{:S(2)}) copy-start(s32[1,128,128]{2,1,0:T(8,128)} %param.16) | copy-start | bytes 196612
  71.2 7.5 %copy-start.3 = (s32[1,128,128]{2,1,0:T(8,128)S(1)}, s32[1,128,128]{2,1,0:T(8,128)}, u32[]{:S(2)}) copy-start(s32[1,128,128]{2,1,0:T(8,128)} %param.15) | copy-start | bytes 196612

commit v2 on v0

v2 whole, which is shorter than its diff:
```python
import functools

import jax
import jax.numpy as jnp
from jax import lax
from jax.experimental import pallas as pl
from jax.experimental.pallas import tpu as pltpu
from jax.sharding import PartitionSpec as P

WIN = 16
LANES = 128
VMEM = pl.BlockSpec(memory_space=pltpu.VMEM)
SMEM = pl.BlockSpec(memory_space=pltpu.SMEM)
LIMIT = 60 * 1024 * 1024


def compose_weights(coef, bases):
    mixed = jnp.einsum(
        "rb,bij->rij", coef, bases.astype(jnp.float32), precision=lax.Precision.HIGHEST
    )
    return mixed.astype(jnp.bfloat16)


def weight_part(bases, self_weight, coef):
    stacked = jnp.concatenate([compose_weights(coef, bases), self_weight[None]], axis=0)
    matrices, pair, width = stacked.shape
    split = stacked.reshape(matrices, pair, width // LANES, LANES).transpose(0, 2, 1, 3)
    return split


MESH = pl.DeviceIdType.MESH
ANY = pl.BlockSpec(memory_space=pl.ANY)
GROUP = 8
FIRST_GROUPS = 4


def rows_of_group(group, send_ref, rows_ref, out_ref):
    slots = send_ref.shape[1]
    nodes, width = rows_ref.shape
    ids = send_ref[pl.ds(pl.multiple_of(group * GROUP, GROUP), GROUP), :]
    hot = (
        (ids[:, :, None] == lax.broadcasted_iota(jnp.int32, (GROUP, slots, nodes), 2))
        .astype(jnp.float32)
        .astype(jnp.bfloat16)
        .reshape(GROUP * slots, nodes)
    )
    got = jnp.dot(hot, rows_ref[...], preferred_element_type=jnp.float32)
    out_ref[pl.ds(group * GROUP, GROUP)] = got.astype(jnp.bfloat16).reshape(GROUP, slots, width)


def remote(src, dst, send_sem, recv_sem, to):
    return pltpu.make_async_remote_copy(
        src_ref=src,
        dst_ref=dst,
        send_sem=send_sem,
        recv_sem=recv_sem,
        device_id=(to,),
        device_id_type=MESH,
    )


def exchange_body(count, with_weights, *refs):
    if with_weights:
        (send_ref, rows_ref, part_ref, in_ref, full_ref, out_ref, send_sem, recv_sem,
         plane_send, plane_recv, far_send, far_recv, core_send, core_recv) = refs
    else:
        send_ref, rows_ref, in_ref, out_ref, send_sem, recv_sem = refs
    me = lax.axis_index("dom")
    groups = count // GROUP
    barrier = pltpu.get_barrier_semaphore()

    def signal(k, carry):
        pl.semaphore_signal(
            barrier, inc=1, device_id=(lax.rem(me + k, count),), device_id_type=MESH
        )
        return carry

    lax.fori_loop(1, count, signal, 0)

    def group_at(t):
        return lax.rem(me // GROUP + 5 * t, groups)

    def compute(t):
        rows_of_group(group_at(t), send_ref, rows_ref, out_ref)

    def send(t, first):
        for i in range(first, GROUP):
            to = group_at(t) * GROUP + lax.rem(me + i, GROUP)
            remote(out_ref.at[to], in_ref.at[me], send_sem, recv_sem, to).start()

    def step(t, carry):
        compute(t + 1)
        send(t, 0)
        return carry

    compute(0)
    compute(1)
    pl.semaphore_wait(barrier, count - 1)
    if with_weights:
        core = lax.rem(me, 2)
        x = lax.rem(me // 2, 4)
        y = lax.rem(me // 8, 4)
        z = me // 32
        pair = lax.rem(me, 8)
        mine = pltpu.make_async_copy(
            part_ref.at[core], full_ref.at[core, :, :, z, y, pair], plane_recv
        )
        mine.start()

        def spread(layer):
            def one(k, carry):
                column = lax.rem(x + k, 4)
                if layer == 0:
                    line = (z * 4 + lax.rem(y + k // 4, 4)) * 4
                else:
                    line = (lax.rem(z + k // 4, 4) * 4 + y) * 4
                remote(
                    part_ref.at[layer],
                    full_ref.at[layer, :, :, z, y, pair],
                    plane_send.at[jnp.where(core == layer, 0, 1)],
                    plane_recv,
                    (line + column) * 2 + layer,
                ).start()
                return carry

            lax.fori_loop(jnp.where(core == layer, 1, 0), 16, one, 0)

        spread(0)
        spread(1)
    send(0, 1)
    if not with_weights:
        lax.fori_loop(1, groups - 1, step, 0)
    else:
        lax.fori_loop(1, FIRST_GROUPS, step, 0)
        arrived = full_ref.at[0, :, :, 0]
        pltpu.make_async_copy(arrived, arrived, plane_recv).wait()

        def far(layer):
            copies = []
            for k in (1, 3, 2):
                if layer == 0:
                    slab = full_ref.at[0, :, :, z]
                    to = lax.rem(me + 32 * k, count)
                else:
                    slab = full_ref.at[1, :, :, :, y]
                    to = z * 32 + lax.rem(y + k, 4) * 8 + pair
                copies.append(remote(slab, slab, far_send.at[k], far_recv.at[k], to))
            return copies

        for layer in range(2):
            @pl.when(core == layer)
            def _():
                for copy in far(layer):
                    copy.start()

        lax.fori_loop(FIRST_GROUPS, groups - 1, step, 0)
    send(groups - 1, 0)
    if with_weights:
        for layer in range(2):
            @pl.when(core == layer)
            def _():
                for copy in far(layer):
                    copy.wait()
        across = remote(
            full_ref.at[core], full_ref.at[core], core_send, core_recv, me + 1 - 2 * core
        )
        across.start()
        across.wait()
        gone = full_ref.at[0, :, :, 0:3, 0, 0:5]
        pltpu.make_async_copy(gone, gone, plane_send.at[0]).wait()
        gone = full_ref.at[0, :, :, 0:2, 0]
        pltpu.make_async_copy(gone, gone, plane_send.at[1]).wait()
    some = pl.ds(0, count - 1)
    pltpu.make_async_copy(in_ref.at[some], in_ref.at[some], recv_sem).wait()
    pltpu.make_async_copy(out_ref.at[some], out_ref.at[some], send_sem).wait()


def exchange(send_rows, rows, part=None):
    count, slots = send_rows.shape
    block = (count, slots, rows.shape[1])
    out_shape = [jax.ShapeDtypeStruct(block, rows.dtype)]
    inputs = [send_rows, rows]
    sems = [pltpu.SemaphoreType.DMA] * 2
    if part is not None:
        layers, matrices, halves, pair, lanes = part.shape
        inputs.append(part)
        out_shape.append(
            jax.ShapeDtypeStruct((layers, matrices, halves, 4, 4, 8, pair, lanes), part.dtype)
        )
        sems += [pltpu.SemaphoreType.DMA((2,)), pltpu.SemaphoreType.DMA]
        sems += [pltpu.SemaphoreType.DMA((4,))] * 2 + [pltpu.SemaphoreType.DMA] * 2
    return pl.pallas_call(
        functools.partial(exchange_body, count, part is not None),
        out_shape=out_shape,
        in_specs=[VMEM] * len(inputs),
        out_specs=[ANY] * len(out_shape),
        scratch_shapes=[pltpu.VMEM(block, rows.dtype)] + sems,
        compiler_params=pltpu.CompilerParams(
            collective_id=0 if part is not None else 1,
            has_side_effects=True,
            vmem_limit_bytes=LIMIT,
        ),
        name="exchange" if part is None else "exchange_weights",
    )(*inputs)


def layer_body(
    relu,
    layer,
    count_ref,
    window_ref,
    source_ref,
    target_ref,
    relation_ref,
    own_hbm,
    recv_hbm,
    weight_hbm,
    bias_ref,
    out_ref,
    table,
    pooled,
    counts,
    stage_a,
    own_ref,
    recv_ref,
    weight_ref,
    own_sem,
    recv_sem,
    weight_sem,
):
    nodes, width = own_ref.shape
    relations = weight_ref.shape[0] - 1
    blocks, block_width = target_ref.shape
    slots = WIN * relations
    chunk = 256
    pieces = recv_sem.shape[0]
    piece = recv_ref.shape[0] // pieces

    own_copy = pltpu.make_async_copy(own_hbm, own_ref, own_sem)
    own_copy.start()
    recv_copies = []
    for p in range(pieces):
        rows = pl.ds(p * piece, piece)
        copy = pltpu.make_async_copy(recv_hbm.at[rows], recv_ref.at[rows], recv_sem.at[p])
        copy.start()
        recv_copies.append(copy)
    weight_copy = pltpu.make_async_copy(weight_hbm.at[layer], weight_ref, weight_sem)
    weight_copy.start()

    def clear(i, carry):
        at = pl.multiple_of(i * slots, slots)
        pooled[pl.ds(at, slots), :] = jnp.zeros((slots, width), jnp.float32)
        counts[pl.ds(at, slots), :] = jnp.zeros((slots, LANES), jnp.float32)
        return carry

    lax.fori_loop(0, nodes // WIN, clear, 0)

    def fill(src_ref, first, last, base):
        def step(i, carry):
            rows = src_ref[pl.ds(pl.multiple_of(i * chunk, chunk), chunk), :].astype(jnp.float32)
            at = pl.multiple_of(base + i * 2 * chunk, 2 * chunk)
            table[pl.ds(at, chunk, stride=2), :] = rows[:, :LANES]
            table[pl.ds(at + 1, chunk, stride=2), :] = rows[:, LANES:]
            return carry

        lax.fori_loop(first, last, step, 0)

    own_copy.wait()
    fill(own_ref, 0, nodes // chunk, 0)
    for p in range(pieces):
        recv_copies[p].wait()
        fill(recv_ref, p * piece // chunk, (p + 1) * piece // chunk, 2 * nodes)

    used = count_ref[0]

    def gather(pair, stage):
        for h in range(2):
            row = source_ref.at[2 * pair + h]
            for e in range(block_width):
                at = pl.multiple_of(row[e], 2)
                stage[pl.ds(2 * (h * block_width + e), 2), :] = table[pl.ds(at, 2), :]

    def pool(pair, stage):
        ids = []
        for h in range(2):
            row = pl.ds(2 * pair + h, 1)
            shift = jnp.where(2 * pair + h < used, h * slots, 2 * slots)
            ids.append(relation_ref[row, :] * WIN + lax.rem(target_ref[row, :], WIN) + shift)
        both = jnp.concatenate(ids, axis=1)
        hot = (
            both == lax.broadcasted_iota(jnp.int32, (2 * slots, 2 * block_width), 0)
        ).astype(jnp.float32).astype(jnp.bfloat16)
        edges = 2 * block_width
        data = jnp.concatenate(
            [
                stage[pl.ds(0, edges, stride=2), :].astype(jnp.bfloat16),
                stage[pl.ds(1, edges, stride=2), :].astype(jnp.bfloat16),
                jnp.ones((edges, LANES), jnp.bfloat16),
            ],
            axis=1,
        )
        got = jnp.dot(hot, data, preferred_element_type=jnp.float32)
        for h in range(2):
            at = pl.multiple_of(window_ref[2 * pair + h] * slots, slots)
            rows = pl.ds(at, slots)
            pooled[rows, :] += got[h * slots : (h + 1) * slots, :width]
            counts[rows, :] += got[h * slots : (h + 1) * slots, width:]

    gather(0, stage_a)

    def pair_step(i, carry):
        pool(i, stage_a)
        gather(jnp.minimum(i + 1, blocks // 2 - 1), stage_a)
        return carry

    lax.fori_loop(0, (used + 1) // 2, pair_step, 0)

    weight_copy.wait()
    part = 256
    windows = part // WIN

    def finish(i, carry):
        at = pl.multiple_of(i * part, part)
        own = own_ref[pl.ds(at, part), :]
        totals = [
            jnp.dot(own, weight_ref[relations, h], preferred_element_type=jnp.float32)
            + bias_ref[:, h * LANES : (h + 1) * LANES]
            for h in range(2)
        ]
        base = pl.multiple_of(i * windows * slots, windows * slots)
        sums = pooled[pl.ds(base, windows * slots), :].reshape(windows, relations, WIN, width)
        tally = counts[pl.ds(base, windows * slots), :].reshape(windows, relations, WIN, LANES)
        for r in range(relations):
            inverse = 1.0 / jnp.maximum(tally[:, r].reshape(part, LANES), 1.0)
            sums_r = sums[:, r].reshape(part, width)
            mean = jnp.concatenate(
                [sums_r[:, :LANES] * inverse, sums_r[:, LANES:] * inverse], axis=1
            ).astype(jnp.bfloat16)
            totals = [
                totals[h] + jnp.dot(mean, weight_ref[r, h], preferred_element_type=jnp.float32)
                for h in range(2)
            ]
        total = jnp.concatenate(totals, axis=1)
        if relu:
            total = jnp.maximum(total, 0.0)
        out_ref[pl.ds(at, part), :] = total.astype(jnp.bfloat16)
        return carry

    lax.fori_loop(0, nodes // part, finish, 0)


def relational_layer(
    layer, rows, received, count, windows, sources, targets, relation_ids, weights, bias
):
    nodes, width = rows.shape
    relations = weights.shape[1] - 1
    table_rows = 2 * (nodes + received.shape[0])
    pieces = 4
    return pl.pallas_call(
        functools.partial(layer_body, layer == 0, layer),
        out_shape=jax.ShapeDtypeStruct((nodes, width), jnp.bfloat16),
        in_specs=[SMEM, SMEM, SMEM, VMEM, VMEM, ANY, ANY, ANY, VMEM],
        out_specs=VMEM,
        scratch_shapes=[
            pltpu.VMEM((table_rows, LANES), jnp.float32),
            pltpu.VMEM((nodes * relations, width), jnp.float32),
            pltpu.VMEM((nodes * relations, LANES), jnp.float32),
            pltpu.VMEM((4 * LANES, LANES), jnp.float32),
            pltpu.VMEM(rows.shape, rows.dtype),
            pltpu.VMEM(received.shape, received.dtype),
            pltpu.VMEM(weights.shape[1:], weights.dtype),
            pltpu.SemaphoreType.DMA,
            pltpu.SemaphoreType.DMA((pieces,)),
            pltpu.SemaphoreType.DMA,
        ],
        compiler_params=pltpu.CompilerParams(vmem_limit_bytes=LIMIT),
        name="relational_layer",
    )(
        count, windows, sources, targets, relation_ids, rows, received, weights,
        bias.reshape(1, width),
    )


def shards(
    features,
    edge_source,
    edge_relation,
    edge_target,
    block_count,
    send_list,
    bases_first,
    self_first,
    coef_first,
    bias_first,
    bases_second,
    self_second,
    coef_second,
    bias_second,
):
    sources = edge_source[0] * 2
    targets = edge_target[0]
    windows = targets[:, 0] // WIN
    send_rows = send_list[0]
    width = features.shape[1]

    part = jnp.stack(
        [
            weight_part(bases_first, self_first, coef_first),
            weight_part(bases_second, self_second, coef_second),
        ]
    )
    received, full = exchange(send_rows, features, part)
    full = full.reshape(full.shape[:3] + (width, LANES))
    hidden = relational_layer(
        0, features, received.reshape(-1, width), block_count, windows, sources, targets,
        edge_relation[0], full, bias_first,
    )
    (received,) = exchange(send_rows, hidden)
    return relational_layer(
        1, hidden, received.reshape(-1, width), block_count, windows, sources, targets,
        edge_relation[0], full, bias_second,
    )


def solution(mesh):
    placed = (
        P("dom", None),
        P("dom", None, None),
        P("dom", None, None),
        P("dom", None, None),
        P("dom"),
        P("dom", None, None),
        P(None, "dom", None),
        P("dom", None),
        P(),
        P(),
        P(None, "dom", None),
        P("dom", None),
        P(),
        P(),
    )
    return jax.shard_map(
        shards, mesh=mesh, in_specs=placed, out_specs=P("dom", None), check_vma=False
    )
```

time: 211 us -> 151 us (0.72)
  the two profiles are of different devices: /device:TPU:86 before, /device:TPU:3 now
where the time goes in v2:
time: 151 us; the launch traced here: 149 us
  Pallas kernels  141 us (93%)
  other arithmetic  3.33 us (2%)
  local copies, waits for them, and re-layouts  2.44 us (2%)
  matrix products  1.72 us (1%)
    pallas_call x2, Pallas kernels, exchange(): pl.pallas_call(functools.partial(exchange_body, count, part is not None),...  83.6 us
    pallas_call x2, Pallas kernels, relational_layer(): pl.pallas_call(functools.partial(layer_body, layer == 0, layer), out_shap...  57 us

profile of v2, /device:TPU:3, one launch (start us, length us, event | category | flops | bytes accessed | tf_op | source)
XLA Modules:
  0.0 148.9 jit_solution(7875561089911683209)
XLA Ops:
  0.0 0.0 copy-start
  0.7 0.9 slice_reduce_fusion
  1.6 0.5 and_select_fusion.window_ref
  2.1 0.0 copy-done
  2.1 0.8 convolution_convert_fusion.1
  3.0 0.9 convolution_convert_fusion
  3.9 0.7 maximum_bitcast_fusion
  4.6 0.6 pad_maximum_fusion.refs_2_
  5.2 1.5 multiply_bitcast_fusion.source_ref
  6.7 1.4 copy.18
  8.2 47.6 %exchange_weights.1 = (bf16[128,32,256]{2,1,0:T(8,128)(2,1)}, bf16[2,9,2,4,4,8,2,128]{7,6,5,4,3,2,1,0:T(2,128)(2,1)}) custom-call(s32[128,32]{1,0:T(8,128)} %bitcast.34, bf16[1024,256]{1,0:T(8,128)(2,1)} %own_hbm.1, bf16[2,9,2,2,128]{4,3,2,1,0:T(2,128)(2,1)} %pad_maximum_fusion.refs_2_), custom_call_target="tpu_custom_call" | custom-call | tf_op jit(solution)/shard_map/exchange_weights/pallas_call | solution.py:192
  55.8 28.5 %relational_layer.2.refs_1_.own_hbm = bf16[1024,256]{1,0:T(8,128)(2,1)} custom-call(s32[1]{0:T(128)S(6)} %copy.27.count_ref, s32[128]{0:T(128)} %and_select_fusion.window_ref, s32[128,128]{1,0:T(8,128)} %multiply_bitcast_fusion.source_ref, s32[128,128]{1,0:T(8,128)} %bitcast.37, s32[128,128]{1,0:T(8,128)} %bitcast.39, bf16[1024,256]{1,0:T(8,128)(2,1)} %own_hbm.1, ...), custom_call_target="tpu_custom_call" | custom-call | tf_op jit(solution)/shard_map/relational_layer/pallas_call | solution.py:359
  84.3 36.0 %exchange.1 = bf16[128,32,256]{2,1,0:T(8,128)(2,1)} custom-call(s32[128,32]{1,0:T(8,128)} %bitcast.35, bf16[1024,256]{1,0:T(8,128)(2,1)} %relational_layer.2.refs_1_.own_hbm), custom_call_target="tpu_custom_call" | custom-call | tf_op jit(solution)/shard_map/exchange/pallas_call | solution.py:192
  120.3 28.5 %relational_layer.3 = bf16[1024,256]{1,0:T(8,128)(2,1)} custom-call(s32[1]{0:T(128)S(6)} %copy.27.count_ref, s32[128]{0:T(128)} %and_select_fusion.window_ref, s32[128,128]{1,0:T(8,128)} %multiply_bitcast_fusion.source_ref, s32[128,128]{1,0:T(8,128)} %bitcast.38, s32[128,128]{1,0:T(8,128)} %bitcast.40, bf16[1024,256]{1,0:T(8,128)(2,1)} %relational_layer.2.refs_1_.own_hbm, ...), custom_call_target="tpu_custom_call" | custom-call | tf_op jit(solution)/shard_map/relational_layer/pallas_call | solution.py:359
  (4 shorter events, 0.0 us)
Async XLA Ops:
  0.0 2.1 %copy-start = (bf16[30,2,256]{2,1,0:T(2,128)(2,1)S(1)}, bf16[30,2,256]{2,1,0:T(2,128)(2,1)}, u32[]{:S(2)}) copy-start(bf16[30,2,256]{2,1,0:T(2,128)(2,1)} %param.20) | copy-start | bytes 92164
